TPU v7x, 128 devices: a whole 4x4x4 slice. The times are simulated.
128 devices in a mesh: ctx: 16 (over x, z), head: 8 (over y, core).
Axes of the slice: x: 4, y: 4, z: 4, core: 2. Of those that a mesh axis runs over, the one named last changes fastest.
Arguments:
- input_x_channels: bfloat16 [16384, 8192], P('ctx', 'head'), may hold values from -4 to 4
- input_b_channels: bfloat16 [16384, 1024], P('ctx', 'head'), may hold values from -3 to 3
- input_c_channels: bfloat16 [16384, 1024], P('ctx', 'head'), may hold values from -3 to 3
- input_gate_channels: bfloat16 [16384, 8192], P('ctx', 'head'), may hold values from -75 to 75
- raw_step_sizes: float32 [128, 16384], P('head', 'ctx'), may hold values from -7 to 800
- log_decay_rate: float32 [128], P('head'), may hold values from -8 to -2.3
- head_skip_coeff: float32 [128], P('head'), may hold values from 0.5 to 2
- x_conv_taps: bfloat16 [4, 8192], P(None, 'head'), may hold values from -3 to 3
- b_conv_taps: bfloat16 [4, 1024], P(None, 'head'), may hold values from -3 to 3
- c_conv_taps: bfloat16 [4, 1024], P(None, 'head'), may hold values from -3 to 3
- gated_norm_gain: bfloat16 [8192], P('head'), may hold values from 0.099609375 to 1.8984375
- output_weight: bfloat16 [8192, 4096], P('head'), may hold values from -0.0625 to 0.0625
- adapter_down_panels: bfloat16 [96, 8192, 64], P('ctx', 'head'), may hold values from -0.0625 to 0.0625
- adapter_up_panels: bfloat16 [96, 64, 4096], P('ctx', None, 'head'), may hold values from -0.75 to 0.75
- turn_first_token: int32 [32], replicated, may hold values from 0 to 16256, as said below
- tenant_of_turn: int32 [32], replicated, may hold values from 0 to 95
- tenant_panel_index: int32 [96], replicated, may hold values from 0 to 95, each once
Outputs:
- out: bfloat16 [16384, 4096], P('ctx', 'head')
Inputs may be any that keep to these rules, and one draw needn't show every extreme that they name: `turn_first_token`: strictly increasing multiples of 128; the first is 0; every aligned block of 1024 tokens holds exactly 2 starts, and in every block but the first the earlier of them lies past the block's first token.
All inputs are finite; a program needn't handle non-finite values.
Results may differ from a plain program's by a relative error of at most 0.014.
Values may be sent and summed in bfloat16 or wider, within the bound.
A program may use at most 128 MiB of HBM per device.

v0:
```python
import jax
import jax.numpy as jnp
from jax import lax
from jax.sharding import PartitionSpec as P

P_SIZE = 64
N = 128
K = 4
Q = 128
TURN_DEV = 2
highest = lax.Precision.HIGHEST
epsilon = 1e-05


def shifted(block, axis, distance):
    devices = range(lax.axis_size(axis))
    route = [(i - distance, i) for i in devices if i - distance in devices]
    return lax.ppermute(block, axis, route)


def conv_rows(sequence, tail_rows, weight):
    token_rows = sequence.shape[0]
    joined = jnp.concatenate([tail_rows, sequence], axis=0).astype(jnp.float32)
    total = jnp.zeros((token_rows, sequence.shape[1]), jnp.float32)
    for tap in range(weight.shape[0]):
        total = total + weight[tap].astype(jnp.float32) * joined[tap : tap + token_rows]
    return jax.nn.silu(total).astype(jnp.bfloat16)


def local(
    input_x_channels,
    input_b_channels,
    input_c_channels,
    input_gate_channels,
    raw_step_sizes,
    log_decay_rate,
    head_skip_coeff,
    x_conv_taps,
    b_conv_taps,
    c_conv_taps,
    gated_norm_gain,
    output_weight,
    adapter_down_panels,
    adapter_up_panels,
    turn_first_token,
    tenant_of_turn,
    tenant_panel_index,
):
    token_rows = input_x_channels.shape[0]
    head_count = log_decay_rate.shape[0]
    group_count = input_b_channels.shape[1] // N
    per_group = head_count // group_count
    conv_edge = K - 1
    conv_tails = shifted(
        (
            input_x_channels[token_rows - conv_edge :],
            input_b_channels[token_rows - conv_edge :],
            input_c_channels[token_rows - conv_edge :],
        ),
        "ctx",
        1,
    )
    x_conv = conv_rows(input_x_channels, conv_tails[0], x_conv_taps)
    b_conv = conv_rows(input_b_channels, conv_tails[1], b_conv_taps)
    c_conv = conv_rows(input_c_channels, conv_tails[2], c_conv_taps)
    block_count = token_rows // Q
    step_sizes = jax.nn.softplus(raw_step_sizes)
    decay_rate = jnp.exp(log_decay_rate)
    step_heads = step_sizes.reshape(head_count, block_count, Q)
    running = jnp.cumsum(-step_heads * decay_rate[:, None, None], axis=2)
    run_blocks = running.transpose(1, 0, 2).reshape(block_count, group_count, per_group, Q)
    step_blocks = step_heads.transpose(1, 0, 2).reshape(block_count, group_count, per_group, Q)
    x_blocks = x_conv.astype(jnp.float32).reshape(block_count, Q, group_count, per_group, P_SIZE)
    b_blocks = b_conv.astype(jnp.float32).reshape(block_count, Q, group_count, N)
    c_blocks = c_conv.astype(jnp.float32).reshape(block_count, Q, group_count, N)
    scores = jnp.einsum("cqgn,ckgn->cgqk", c_blocks, b_blocks, precision=highest)
    causal = jnp.arange(Q)[:, None] >= jnp.arange(Q)[None, :]
    log_gap = run_blocks[..., :, None] - run_blocks[..., None, :]
    decay_mat = jnp.where(causal, jnp.exp(jnp.where(causal, log_gap, 0.0)), 0.0)
    mixing = scores[:, :, None] * decay_mat * step_blocks[..., None, :]
    y_local = jnp.einsum("cghqk,ckghp->cqghp", mixing, x_blocks, precision=highest)
    tail_weight = jnp.exp(run_blocks[..., -1:] - run_blocks) * step_blocks
    block_states = jnp.einsum(
        "cghk,ckghp,ckgn->cghpn", tail_weight, x_blocks, b_blocks, precision=highest
    )
    block_log = run_blocks[..., -1]

    def carry_step(carried, inputs):
        fresh_state, step_log = inputs
        return (jnp.exp(step_log)[..., None, None] * carried + fresh_state, carried)

    empty_state = jnp.zeros((group_count, per_group, P_SIZE, N), jnp.float32)
    device_state, before = lax.scan(carry_step, empty_state, (block_states, block_log))
    device_log = jnp.sum(block_log, axis=0)
    run_tokens = run_blocks.transpose(0, 3, 1, 2)
    y_local = y_local + jnp.exp(run_tokens)[..., None] * jnp.einsum(
        "cqgn,cghpn->cqghp", c_blocks, before, precision=highest
    )
    all_logs, states = (
        lax.all_gather(device_log[None], "ctx", axis=0, tiled=True),
        lax.all_gather(device_state[None], "ctx", axis=0, tiled=True),
    )
    device_count = all_logs.shape[0]
    own_index = lax.axis_index("ctx")
    order_index = jnp.arange(device_count)
    between = (order_index[:, None] < order_index[None, :]) & (order_index[None, :] < own_index)
    span_log = jnp.einsum("jk,kgh->jgh", between.astype(jnp.float32), all_logs, precision=highest)
    weights = jnp.where((order_index < own_index)[:, None, None], jnp.exp(span_log), 0.0)
    incoming = jnp.einsum("jgh,jghpn->ghpn", weights, states, precision=highest)
    start_log = jnp.cumsum(block_log, axis=0) - block_log
    device_running = start_log[:, None] + run_tokens
    y_value = y_local + jnp.exp(device_running)[..., None] * jnp.einsum(
        "cqgn,ghpn->cqghp", c_blocks, incoming, precision=highest
    )
    y_value = y_value + head_skip_coeff.reshape(group_count, per_group)[:, :, None] * x_blocks
    group_width = per_group * P_SIZE
    gated = y_value.reshape(token_rows, group_count, group_width) * jax.nn.silu(
        input_gate_channels.astype(jnp.float32)
    ).reshape(token_rows, group_count, group_width)
    norm_scale = lax.rsqrt(jnp.mean(gated * gated, axis=2, keepdims=True) + epsilon)
    y_normed = (
        (gated * norm_scale).reshape(token_rows, -1) * gated_norm_gain.astype(jnp.float32)
    ).astype(jnp.bfloat16)
    own_index = lax.axis_index("ctx")
    slot_count = TURN_DEV + 1
    slot_turns = TURN_DEV * own_index - 1 + jnp.arange(slot_count)
    clipped = jnp.maximum(slot_turns, 0)
    tenants = jnp.take(tenant_of_turn, clipped)
    slot_homes = jnp.take(tenant_panel_index, tenants)
    all_down, all_up = (
        lax.all_gather(adapter_down_panels, "ctx", axis=0, tiled=True),
        lax.all_gather(adapter_up_panels, "ctx", axis=0, tiled=True),
    )
    down_slots = jnp.take(all_down, slot_homes, axis=0)
    up_slots = jnp.take(all_up, slot_homes, axis=0)
    base_out = lax.psum_scatter(
        jnp.dot(y_normed, output_weight, preferred_element_type=jnp.float32).astype(jnp.bfloat16),
        "head",
        scatter_dimension=1,
        tiled=True,
    ).astype(jnp.float32)
    own_starts = lax.dynamic_slice_in_dim(turn_first_token, TURN_DEV * own_index, TURN_DEV, 0)
    token_place = own_index * token_rows + jnp.arange(token_rows)
    token_slot = jnp.sum((token_place[:, None] >= own_starts[None, :]).astype(jnp.int32), axis=1)
    slot_mask = (token_slot[:, None] == jnp.arange(slot_count)[None, :]).astype(jnp.float32)
    low_slots = jnp.einsum("tc,scr->tsr", y_normed, down_slots, preferred_element_type=jnp.float32)
    rank_reduced = jnp.sum(low_slots * slot_mask[:, :, None], axis=1)
    rank_reduced = lax.psum(rank_reduced, "head").astype(jnp.bfloat16)
    adapter_out = jnp.einsum(
        "tr,srd->tsd", rank_reduced, up_slots, preferred_element_type=jnp.float32
    )
    adapter_out = jnp.sum(adapter_out * slot_mask[:, :, None], axis=1)
    return (base_out + adapter_out).astype(jnp.bfloat16)


def solution(mesh):
    in_specs = (
        P("ctx", "head"),
        P("ctx", "head"),
        P("ctx", "head"),
        P("ctx", "head"),
        P("head", "ctx"),
        P("head"),
        P("head"),
        P(None, "head"),
        P(None, "head"),
        P(None, "head"),
        P("head"),
        P("head", None),
        P("ctx", "head", None),
        P("ctx", None, "head"),
        P(),
        P(),
        P(),
    )
    out_specs = P("ctx", "head")
    return jax.shard_map(local, mesh=mesh, in_specs=in_specs, out_specs=out_specs, check_vma=False)
```

profile of v0, /device:TPU:0, one launch (start us, length us, event | category | flops | bytes accessed | tf_op | source)
XLA Modules:
  0.0 349.8 jit_solution(5705735439827553091)
XLA Ops:
  7.3 0.9 copy.74
  8.2 3.9 %collective-permute-start = (bf16[3,1024]{0,1:T(8,128)(2,1)}, bf16[3,1024]{0,1:T(8,128)(2,1)S(1)}, u32[]{:S(2)}, u32[]{:S(2)}) collective-permute-start(bf16[3,1024]{0,1:T(8,128)(2,1)} %copy.74), channel_id=1, source_target_pairs={{0,8},{8,16},{16,24},{24,32},{32,40},{40,48},{48,56},{56,64},{64,7... | collective-permute-start | bytes 18440 | tf_op jit(solution)/shard_map/ppermute | solution.py:18
  12.8 3.8 %collective-permute-start.2 = (bf16[3,128]{1,0:T(4,128)(2,1)S(1)}, bf16[3,128]{1,0:T(4,128)(2,1)S(1)}, u32[]{:S(2)}, u32[]{:S(2)}) collective-permute-start(bf16[3,128]{1,0:T(4,128)(2,1)S(1)} %slice.104), channel_id=1, source_target_pairs={{0,8},{8,16},{16,24},{24,32},{32,40},{40,48},{48,56},{56,64},{64,7... | collective-permute-start | bytes 2312 | tf_op jit(solution)/shard_map/ppermute | solution.py:18
  16.6 0.9 slice_convert_fusion.3
  17.5 0.9 fusion.48
  19.1 4.5 %reduce_window_sum.22 = f32[16,8,128]{2,1,0:T(8,128)S(1)} reduce-window(f32[16,8,128]{2,1,0:T(8,128)S(1)} %negate_multiply_fusion, f32[]{:T(128)} %constant.95.clone.1), window={size=1x1x128 pad=0_0x0_0x127_0}, to_apply=%region_0.1 | reduce-window | flops 2080768 | bytes 131076 | tf_op jit(solution)/shard_map/jit(cumsum)/reduce_window_sum | solution.py:70
  25.0 2.9 copy.75
  28.5 1.2 maximum_convert_fusion
  29.7 5.5 %convert_bitcast_fusion = (f32[128,8,8,128]{3,1,2,0:T(8,128)}, bf16[1024,1024]{0,1:T(8,128)(2,1)S(1)}) fusion(f32[1027,1024]{0,1:T(8,128)S(1)} %maximum_convert_fusion, f32[1024]{0:T(1024)S(1)} %bitcast.186, f32[1024]{0:T(1024)S(1)} %bitcast.187, f32[1024]{0:T(1024)S(1)} %bitcast.185, f32[1024]{0:T(1024)S(1)} %bitcast.184), kind=kLoop, calls=%fused_computation.43 | loop fusion | flops 13631488 | bytes 23085056
  36.2 3.8 %fusion.31 = f32[8,1,16,64,128]{4,3,2,1,0:T(8,128)} fusion(bf16[8,128,128,1]{2,1,3,0:T(8,128)(2,1)S(1)} %bitcast.173, f32[8,128,16,64]{1,0,3,2:T(8,128)S(1)} %convert_multiply_fusion.1), kind=kOutput, calls=%fused_computation.55 | convolution fusion | flops 1610612736 | bytes 8650752 | tf_op jit(solution)/shard_map/cghk,ckghp,ckgn->cghpn/dot_general | solution.py:83
  40.0 16.3 %while.13 = (s32[]{:T(128)}, f32[1,16,64,128]{3,2,1,0:T(8,128)S(1)}, f32[8,1,16,64,128]{4,3,2,1,0:T(8,128)}, f32[8,1,16]{2,1,0:T(1,128)S(1)}, f32[8,1,16,64,128]{4,3,2,1,0:T(8,128)}, /*index=5*/s32[]{:T(128)}, s32[]{:T(128)}) while((s32[]{:T(128)}, f32[1,16,64,128]{3,2,1,0:T(8,128)S(1)}, f32[8,1,16,64,128]{4,3,2,1,0:T(8,128)}, ...), condition=%wide.region_2.3_spmd.clone, body=%wide.region_1.2_spmd.clone.sunk | while | flops 524291 | bytes 2622240 | solution.py:93
  40.9 1.2 bitcast_add_fusion.2
  42.0 0.9 bitcast_dynamic-update-slice_fusion.2
  42.9 1.2 bitcast_add_fusion.2
  44.1 0.9 bitcast_dynamic-update-slice_fusion.2
  45.0 1.2 bitcast_add_fusion.2
  46.1 0.8 bitcast_dynamic-update-slice_fusion.2
  47.0 1.2 bitcast_add_fusion.2
  48.2 0.8 bitcast_dynamic-update-slice_fusion.2
  49.0 1.2 bitcast_add_fusion.2
  50.2 0.9 bitcast_dynamic-update-slice_fusion.2
  51.1 1.2 bitcast_add_fusion.2
  52.3 0.9 bitcast_dynamic-update-slice_fusion.2
  53.1 1.2 bitcast_add_fusion.2
  55.1 1.2 bitcast_add_fusion.2
  58.7 3.5 %collective-permute-start.1 = (bf16[3,128]{1,0:T(4,128)(2,1)S(1)}, bf16[3,128]{1,0:T(4,128)(2,1)S(1)}, u32[]{:S(2)}, u32[]{:S(2)}) collective-permute-start(bf16[3,128]{1,0:T(4,128)(2,1)S(1)} %slice.95), channel_id=1, source_target_pairs={{0,8},{8,16},{16,24},{24,32},{32,40},{40,48},{48,56},{56,64},{64,7... | collective-permute-start | bytes 2312 | tf_op jit(solution)/shard_map/ppermute | solution.py:18
  63.9 36.2 %all-reduce = f32[256]{0:T(256)S(1)} all-reduce(f32[256]{0:T(256)S(1)} %dynamic-update-slice), channel_id=2, replica_groups=mesh['ctx'=16,'head'=8] {'ctx'}, use_global_device_ids=true, to_apply=%add | all-reduce | flops 256 | bytes 2048
  100.7 4.0 %copy.92 = bf16[1024,1024]{0,1:T(8,128)(2,1)} copy(bf16[1024,1024]{1,0:T(8,128)(2,1)} %param.22) | data formatting | bytes 4194304 | tf_op args[3]
  105.4 1.5 copy-done.3
  106.9 3.0 copy.104
  110.1 3.5 %fusion.21 = f32[8,16,64,128]{3,2,1,0:T(8,128)} fusion(bf16[8,128,128,1]{2,1,3,0:T(8,128)(2,1)S(1)} %bitcast.170, f32[8,1,16,64,128]{4,3,2,1,0:T(8,128)S(1)} %copy-done.8), kind=kOutput, calls=%fused_computation.38 | convolution fusion | flops 1610612736 | bytes 8650752 | tf_op jit(solution)/shard_map/cqgn,cghpn->cqghp/dot_general | solution.py:96
  113.6 11.3 %fusion.4 = f32[8,16,64,128]{3,2,1,0:T(8,128)} fusion(f32[8,16,128]{2,1,0:T(8,128)S(1)} %copy.78, f32[8,16,128]{2,1,0:T(8,128)S(1)} %copy.76, f32[8,128,128]{2,1,0:T(8,128)S(1)} %fusion.61, pred[128,128]{1,0:T(8,128)(4,1)S(1)} %iota_compare_fusion, bf16[8,128,16,64]{1,0,3,2:T(8,128)(2,1)S(1)} %bitcast.167), kind=kOutput, calls=%fused_computation.11 | convolution fusion | flops 1621098496 | bytes 6963200 | tf_op jit(solution)/shard_map/cghqk,ckghp->cqghp/dot_general | solution.py:81
  124.9 3.8 %all-gather.10.cloned.1.call-done = f32[16,16,64,128]{3,2,1,0:T(8,128)} async-done(((f32[1,16,64,128]{3,2,1,0:T(8,128)}), f32[16,16,64,128]{3,2,1,0:T(8,128)}) %all-gather.10.cloned.1.call-update) | async-done | bytes 8388624 | tf_op jit(solution)/shard_map/all_gather | solution.py:101
  128.7 12.8 %fusion.2 = f32[16,1,64,128]{3,1,2,0:T(1,128)S(1)} fusion(f32[16,16,1,1]{0,2,3,1:T(1,128)S(1)} %copy.96, f32[16,16,64,128]{3,2,1,0:T(8,128)} %all-gather.10.cloned.1.call-done), kind=kOutput, calls=%fused_computation.9 | convolution fusion | flops 25165824 | bytes 8913920 | tf_op jit(solution)/shard_map/jgh,jghpn->ghpn/dot_general | solution.py:109
  141.5 5.1 %fusion.19 = f32[8,128,1,16,64]{1,4,3,0,2:T(8,128)S(1)} fusion(f32[8,16,64,128]{3,2,1,0:T(8,128)S(1)} %copy-done.6, f32[8,16,64,128]{3,2,1,0:T(8,128)} %fusion.4, f32[8,128,1,16,64]{1,0,4,3,2:T(8,128)S(1)} %bitcast.164, f32[16,64,128,1]{2,1,0,3:T(8,128)S(1)} %bitcast.175, bf16[8,128,128,1]{2,1,3,0:T(8,128)(2,1)S(1)} %bitcast.171, f32[16]{0:T(128)S(1)} %copy-done.13, ...), kind=kOutput, calls=%fused_computation.35 | convolution fusion | flops 1616904192 | bytes 17694784 | tf_op jit(solution)/shard_map/cqgn,ghpn->cqghp/dot_general | solution.py:112
  146.6 3.3 copy.91
  150.0 1.7 multiply_reduce_fusion.1
  151.8 2.0 copy-done.4
  153.8 11.5 %convolution_convert_fusion = bf16[1024,4096]{1,0:T(8,128)(2,1)} fusion(bf16[1024,4096]{1,0:T(8,128)(2,1)S(1)} %bitcast.189, f32[1024,1024]{0,1:T(8,128)S(1)} %get-tuple-element.84, f32[1024]{0:T(1024)S(1)} %convert_element_type.84, f32[1024]{0:T(1024)S(1)} %add_rsqrt_fusion), kind=kOutput, calls=%fused_computation.18 | convolution fusion | flops 8597274624 | bytes 20979712 | tf_op jit(solution)/shard_map/dot_general | solution.py:137
  166.9 24.9 %all-gather.8.cloned.1.call-done = bf16[96,64,512]{2,1,0:T(8,128)(2,1)} async-done(((bf16[6,64,512]{2,1,0:T(8,128)(2,1)}), bf16[96,64,512]{2,1,0:T(8,128)(2,1)}) %all-gather.8.cloned.1.call-update) | async-done | bytes 6291472 | tf_op jit(solution)/shard_map/all_gather | solution.py:132
  191.8 3.3 gather_fusion.3
  195.1 88.6 %all-gather.6.cloned.1.call-done = bf16[96,1024,64]{1,2,0:T(8,128)(2,1)} async-done(((bf16[6,1024,64]{1,2,0:T(8,128)(2,1)}), bf16[96,1024,64]{1,2,0:T(8,128)(2,1)}) %all-gather.6.cloned.1.call-update) | async-done | bytes 12582928 | tf_op jit(solution)/shard_map/all_gather | solution.py:131
  283.7 5.1 %gather_fusion.2 = bf16[3,1024,64]{1,2,0:T(8,128)(2,1)S(1)} fusion(bf16[96,1024,64]{1,2,0:T(8,128)(2,1)} %all-gather.6.cloned.1.call-done, s32[1024]{0:T(1024)S(1)} %pad_clamp_fusion), kind=kCustom, calls=%fused_computation.2 | custom fusion | bytes 786444 | tf_op jit(solution)/shard_map/jit(_take)/gather | solution.py:134
  289.0 2.9 fusion.59
  291.9 31.3 %all-reduce.2 = bf16[1024,64]{0,1:T(8,128)(2,1)S(1)} all-reduce(f32[1024,64]{0,1:T(8,128)S(1)} %multiply_reduce_fusion.2), channel_id=1, replica_groups=mesh['ctx'=16,'head'=8] {'head'}, use_global_device_ids=true, to_apply=%region_9.10 | all-reduce | flops 65536 | bytes 393216 | tf_op jit(solution)/shard_map/psum | solution.py:148
  323.2 1.0 multiply_reduce_fusion
  324.3 16.4 %reduce-scatter.2.cloned.1.call-done = bf16[1024,512]{1,0:T(8,128)(2,1)} async-done(((bf16[1024,4096]{1,0:T(8,128)(2,1)}), bf16[1024,512]{1,0:T(8,128)(2,1)}) %reduce-scatter.2.cloned.1.call-update) | async-done | bytes 1048592 | tf_op jit(solution)/shard_map/reduce_scatter | solution.py:136
  340.7 2.6 add_convert_fusion
  (110 shorter events, 13.2 us)
Async XLA Ops:
  6.5 158.8 %copy-start = (s32[32]{0:T(128)S(1)}, s32[32]{0:T(128)}, u32[]{:S(2)}) copy-start(s32[32]{0:T(128)} %param.34) | copy-start | bytes 388
  6.5 21.5 %copy-start.9 = (bf16[1024,128]{1,0:T(8,128)(2,1)S(1)}, bf16[1024,128]{1,0:T(8,128)(2,1)}, u32[]{:S(2)}) copy-start(bf16[1024,128]{1,0:T(8,128)(2,1)} %param.20) | copy-start | bytes 786436
  6.5 122.1 %all-gather.10.cloned.1.call-start = ((), (), s32[]{:S(2)}) async-start(), calls=%async_computation.4 | async-start | bytes 8912896 | tf_op jit(solution)/shard_map/all_gather | solution.py:101
  8.2 20.3 %collective-permute-start = (bf16[3,1024]{0,1:T(8,128)(2,1)}, bf16[3,1024]{0,1:T(8,128)(2,1)S(1)}, u32[]{:S(2)}, u32[]{:S(2)}) collective-permute-start(bf16[3,1024]{0,1:T(8,128)(2,1)} %copy.74), channel_id=1, source_target_pairs={{0,8},{8,16},{16,24},{24,32},{32,40},{40,48},{48,56},{56,64},{64,7... | collective-permute-start | bytes 18440 | tf_op jit(solution)/shard_map/ppermute | solution.py:18
  12.8 15.2 %collective-permute-start.2 = (bf16[3,128]{1,0:T(4,128)(2,1)S(1)}, bf16[3,128]{1,0:T(4,128)(2,1)S(1)}, u32[]{:S(2)}, u32[]{:S(2)}) collective-permute-start(bf16[3,128]{1,0:T(4,128)(2,1)S(1)} %slice.104), channel_id=1, source_target_pairs={{0,8},{8,16},{16,24},{24,32},{32,40},{40,48},{48,56},{56,64},{64,7... | collective-permute-start | bytes 2312 | tf_op jit(solution)/shard_map/ppermute | solution.py:18
  40.0 18.7 %copy-start.10 = (bf16[1024,128]{1,0:T(8,128)(2,1)S(1)}, bf16[1024,128]{1,0:T(8,128)(2,1)}, u32[]{:S(2)}) copy-start(bf16[1024,128]{1,0:T(8,128)(2,1)} %param.21) | copy-start | bytes 786436
  40.0 22.2 %copy-start.15 = (u32[128]{0:T(128)S(1)}, u32[128]{0:T(128)}, u32[]{:S(2)}) copy-start(u32[128]{0:T(128)} %constant.114) | copy-start | bytes 1540
  40.0 60.3 %copy-start.11 = (bf16[4,128]{1,0:T(4,128)(2,1)S(1)}, bf16[4,128]{1,0:T(4,128)(2,1)}, u32[]{:S(2)}) copy-start(bf16[4,128]{1,0:T(4,128)(2,1)} %param.28) | copy-start | bytes 3076
  56.3 0.8 copy-start.2
  56.3 48.3 %copy-start.12 = (bf16[1024]{0:T(1024)(128)(2,1)S(1)}, bf16[1024]{0:T(1024)(128)(2,1)}, u32[]{:S(2)}) copy-start(bf16[1024]{0:T(1024)(128)(2,1)} %param.29) | copy-start | bytes 6148
  57.1 134.6 %all-gather.8.cloned.1.call-start = ((), (), s32[]{:S(2)}) async-start(), calls=%async_computation.3 | async-start | bytes 6684672 | tf_op jit(solution)/shard_map/all_gather | solution.py:132
  57.9 225.8 %all-gather.6.cloned.1.call-start = ((), (), s32[]{:S(2)}) async-start(), calls=%async_computation.2 | async-start | bytes 13369344 | tf_op jit(solution)/shard_map/all_gather | solution.py:131
  58.6 282.1 %reduce-scatter.2.cloned.1.call-start = ((), (), s32[]{:S(2)}) async-start(), calls=%async_computation.1 | async-start | bytes 9437184 | tf_op jit(solution)/shard_map/reduce_scatter | solution.py:136
  58.7 46.0 %collective-permute-start.1 = (bf16[3,128]{1,0:T(4,128)(2,1)S(1)}, bf16[3,128]{1,0:T(4,128)(2,1)S(1)}, u32[]{:S(2)}, u32[]{:S(2)}) collective-permute-start(bf16[3,128]{1,0:T(4,128)(2,1)S(1)} %slice.95), channel_id=1, source_target_pairs={{0,8},{8,16},{16,24},{24,32},{32,40},{40,48},{48,56},{56,64},{64,7... | collective-permute-start | bytes 2312 | tf_op jit(solution)/shard_map/ppermute | solution.py:18
  104.6 2.2 copy-start.3
  106.9 3.2 copy-start.8
  124.9 16.7 %copy-start.13 = (f32[16]{0:T(128)S(1)}, f32[16]{0:T(128)}, u32[]{:S(2)}) copy-start(f32[16]{0:T(128)} %param.25) | copy-start | bytes 196
  128.7 12.9 %copy-start.5 = (f32[128,8,8,128]{3,2,1,0:T(8,128)S(1)}, f32[128,8,8,128]{3,2,1,0:T(8,128)}, u32[]{:S(2)}) copy-start(f32[128,8,8,128]{3,2,1,0:T(8,128)} %copy.104) | copy-start | bytes 12582916
  128.7 12.9 %copy-start.6 = (f32[8,16,64,128]{3,2,1,0:T(8,128)S(1)}, f32[8,16,64,128]{3,2,1,0:T(8,128)}, u32[]{:S(2)}) copy-start(f32[8,16,64,128]{3,2,1,0:T(8,128)} %fusion.21) | copy-start | bytes 12582916
  146.6 3.3 copy-start.7
  146.6 7.2 %slice-start = ((s8[8388608]{0:T(1024)(128)(4,1)}), s8[4194304]{0:T(1024)(128)(4,1)S(1)}, s32[]{:S(2)}) async-start(s8[8388608]{0:T(1024)(128)(4,1)} %bitcast.188), calls=%async_computation.5 | async-start | bytes 8388608
  150.0 3.8 %slice-start.1 = ((s8[8388608]{0:T(1024)(128)(4,1)}), s8[4194304]{0:T(1024)(128)(4,1)S(1)}, s32[]{:S(2)}) async-start(s8[8388608]{0:T(1024)(128)(4,1)} %bitcast.188), calls=%async_computation.6 | async-start | bytes 8388608
  151.7 2.0 copy-start.4
  165.3 0.7 copy-start.1
  165.3 1.4 copy-start.14
Sparse Core Ops, SparseCore 0:
  57.3 71.3 all-gather.9
  130.8 60.8 all-gather.7
  194.0 89.7 all-gather.5
  286.0 54.6 reduce-scatter.1
where the time goes:
time: 351 us; the launch traced here: 350 us
  waiting for transfers between devices  135 us (38%)
  blocking collectives  67.5 us (19%)
  matrix products  52.3 us (15%)
  other arithmetic  36.4 us (10%)
  local copies, waits for them, and re-layouts  32.7 us (9%)
  between operations  14.3 us (4%)
  starting transfers between devices  11.4 us (3%)
    all_gather x1, waiting for transfers between devices, local(): lax.all_gather(adapter_down_panels, 'ctx', axis=0, tiled=True)  88.6 us
    unnamed x1, blocking collectives  36.2 us
    psum x1, blocking collectives, local(): rank_reduced = lax.psum(rank_reduced, 'head').astype(jnp.bfloat16)  31.3 us
    all_gather x1, waiting for transfers between devices, local(): lax.all_gather(adapter_up_panels, 'ctx', axis=0, tiled=True)  24.9 us
    reduce_scatter x1, waiting for transfers between devices, local(): lax.psum_scatter(jnp.dot(y_normed, output_weight, preferred_element_type=...  16.4 us
    unnamed x44, local copies, waits for them, and re-layouts  15.9 us
    dot_general x1, matrix products, local(): incoming = jnp.einsum('jgh,jghpn->ghpn', weights, states, precision=highest)  12.8 us
    dot_general x1, matrix products, local(): jnp.dot(y_normed, output_weight, preferred_element_type=jnp.float32)  11.5 us
  transfers between devices with their start and end apart: 7, of which 4 were waited for; matrix products, arithmetic and copies ran while one was open for 24% of the time, Pallas kernels for 0%

commit v1 on v0

--- a/solution.py
+++ b/solution.py
@@ -46,6 +46,20 @@
     tenant_of_turn,
     tenant_panel_index,
 ):
+
+    def leaves_divide(tile_in, pos_dim=0):
+        bus_axis = "ctx"
+        cores_n = lax.psum(1, axis_name=bus_axis)
+        in_order = [cores_n if nth == pos_dim else 1 for nth in range(tile_in.ndim)]
+        r2 = lax.all_to_all(
+            jnp.tile(tile_in, in_order),
+            axis_name=bus_axis,
+            split_axis=pos_dim,
+            concat_axis=pos_dim,
+            tiled=True,
+        )
+        return r2
+
     token_rows = input_x_channels.shape[0]
     head_count = log_decay_rate.shape[0]
     group_count = input_b_channels.shape[1] // N
@@ -129,7 +143,7 @@
     slot_homes = jnp.take(tenant_panel_index, tenants)
     all_down, all_up = (
         lax.all_gather(adapter_down_panels, "ctx", axis=0, tiled=True),
-        lax.all_gather(adapter_up_panels, "ctx", axis=0, tiled=True),
+        leaves_divide(adapter_up_panels),
     )
     down_slots = jnp.take(all_down, slot_homes, axis=0)
     up_slots = jnp.take(all_up, slot_homes, axis=0)

time: 351 us -> 367 us (1.046)
  starting transfers between devices: 11.4 us -> 17.3 us
  local copies, waits for them, and re-layouts: 32.7 us -> 37.7 us
    all_to_all x0 -> x1, waiting for transfers between devices: none -> 128 us  [leaves_divide(): lax.all_to_all(jnp.tile(tile_in, in_order), axis_name=bus_axis, split_axi...]
    all_gather x1, waiting for transfers between devices: 88.6 us -> 0.02 us  [local(): lax.all_gather(adapter_down_panels, 'ctx', axis=0, tiled=True)]
    all_gather x1 -> x0, waiting for transfers between devices: 24.9 us -> none  [local(): lax.all_gather(adapter_up_panels, 'ctx', axis=0, tiled=True)]
    reduce_scatter x1, waiting for transfers between devices: 16.4 us -> 0.02 us  [local(): lax.psum_scatter(jnp.dot(y_normed, output_weight, preferred_element_type=...]
    all_to_all x0 -> x1, starting transfers between devices: none -> 5.94 us  [leaves_divide(): lax.all_to_all(jnp.tile(tile_in, in_order), axis_name=bus_axis, split_axi...]
    unnamed x44 -> x54, local copies, waits for them, and re-layouts: 15.9 us -> 17.3 us
  transfers between devices with their start and end apart: 7 -> 7, of which waited for: 4 -> 2; matrix products, arithmetic and copies ran while one was open for 24% -> 25% of each run, Pallas kernels for 0% -> 0%
where the time goes in v1:
time: 367 us; the launch traced here: 363 us
  waiting for transfers between devices  134 us (37%)
  blocking collectives  67.6 us (18%)
  matrix products  52.6 us (14%)
  other arithmetic  39.6 us (11%)
  local copies, waits for them, and re-layouts  37.7 us (10%)
  starting transfers between devices  17.3 us (5%)
  between operations  14.3 us (4%)
    all_to_all x1, waiting for transfers between devices, leaves_divide(): lax.all_to_all(jnp.tile(tile_in, in_order), axis_name=bus_axis, split_axi...  128 us
    unnamed x1, blocking collectives  36.2 us
    psum x1, blocking collectives, local(): rank_reduced = lax.psum(rank_reduced, 'head').astype(jnp.bfloat16)  31.4 us
    unnamed x54, local copies, waits for them, and re-layouts  17.3 us
    dot_general x1, matrix products, local(): incoming = jnp.einsum('jgh,jghpn->ghpn', weights, states, precision=highest)  12.8 us
    dot_general x1, matrix products, local(): jnp.dot(y_normed, output_weight, preferred_element_type=jnp.float32)  11.5 us
    dot_general x1, matrix products, local(): jnp.einsum('cghqk,ckghp->cqghp', mixing, x_blocks, precision=highest)  11.3 us
    ppermute x3, starting transfers between devices, shifted(): return lax.ppermute(block, axis, route)  11.2 us
  transfers between devices with their start and end apart: 7, of which 2 were waited for; matrix products, arithmetic and copies ran while one was open for 25% of the time, Pallas kernels for 0%

profile of v1, /device:TPU:0, one launch (start us, length us, event | category | flops | bytes accessed | tf_op | source)
XLA Modules:
  0.0 362.9 jit_solution(10238147997212758289)
XLA Ops:
  7.3 0.9 copy.74
  8.2 3.9 %collective-permute-start = (bf16[3,1024]{0,1:T(8,128)(2,1)}, bf16[3,1024]{0,1:T(8,128)(2,1)S(1)}, u32[]{:S(2)}, u32[]{:S(2)}) collective-permute-start(bf16[3,1024]{0,1:T(8,128)(2,1)} %copy.74), channel_id=1, source_target_pairs={{0,8},{8,16},{16,24},{24,32},{32,40},{40,48},{48,56},{56,64},{64,7... | collective-permute-start | bytes 18440 | tf_op jit(solution)/shard_map/ppermute | solution.py:18
  12.8 3.8 %collective-permute-start.2 = (bf16[3,128]{1,0:T(4,128)(2,1)S(1)}, bf16[3,128]{1,0:T(4,128)(2,1)S(1)}, u32[]{:S(2)}, u32[]{:S(2)}) collective-permute-start(bf16[3,128]{1,0:T(4,128)(2,1)S(1)} %slice.104), channel_id=1, source_target_pairs={{0,8},{8,16},{16,24},{24,32},{32,40},{40,48},{48,56},{56,64},{64,7... | collective-permute-start | bytes 2312 | tf_op jit(solution)/shard_map/ppermute | solution.py:18
  16.6 1.5 slice_convert_fusion.3
  18.1 0.9 fusion.48
  19.7 4.5 %reduce_window_sum.22 = f32[16,8,128]{2,1,0:T(8,128)S(1)} reduce-window(f32[16,8,128]{2,1,0:T(8,128)S(1)} %negate_multiply_fusion, f32[]{:T(128)} %constant.95.clone.1), window={size=1x1x128 pad=0_0x0_0x127_0}, to_apply=%region_0.1 | reduce-window | flops 2080768 | bytes 131076 | tf_op jit(solution)/shard_map/jit(cumsum)/reduce_window_sum | solution.py:84
  24.2 0.9 slice_reduce_fusion
  26.0 1.4 bitcast_convert_fusion.3
  27.4 2.9 copy.75
  30.5 1.0 multiply_convert_fusion.2
  31.5 1.2 maximum_convert_fusion
  32.8 5.5 %convert_bitcast_fusion = (f32[128,8,8,128]{3,1,2,0:T(8,128)}, bf16[1024,1024]{0,1:T(8,128)(2,1)S(1)}) fusion(f32[1027,1024]{0,1:T(8,128)S(1)} %maximum_convert_fusion, f32[1024]{0:T(1024)S(1)} %bitcast.188, f32[1024]{0:T(1024)S(1)} %bitcast.189, f32[1024]{0:T(1024)S(1)} %bitcast.187, f32[1024]{0:T(1024)S(1)} %bitcast.186), kind=kLoop, calls=%fused_computation.43 | loop fusion | flops 13631488 | bytes 23085056
  39.6 3.8 %fusion.31 = f32[8,1,16,64,128]{4,3,2,1,0:T(8,128)} fusion(bf16[8,128,128,1]{2,1,3,0:T(8,128)(2,1)S(1)} %bitcast.175, f32[8,128,16,64]{1,0,3,2:T(8,128)S(1)} %convert_multiply_fusion.1), kind=kOutput, calls=%fused_computation.55 | convolution fusion | flops 1610612736 | bytes 8650752 | tf_op jit(solution)/shard_map/cghk,ckghp,ckgn->cghpn/dot_general | solution.py:97
  43.4 16.3 %while.13 = (s32[]{:T(128)}, f32[1,16,64,128]{3,2,1,0:T(8,128)S(1)}, f32[8,1,16,64,128]{4,3,2,1,0:T(8,128)}, f32[8,1,16]{2,1,0:T(1,128)S(1)}, f32[8,1,16,64,128]{4,3,2,1,0:T(8,128)}, /*index=5*/s32[]{:T(128)}, s32[]{:T(128)}) while((s32[]{:T(128)}, f32[1,16,64,128]{3,2,1,0:T(8,128)S(1)}, f32[8,1,16,64,128]{4,3,2,1,0:T(8,128)}, ...), condition=%wide.region_2.3_spmd.clone, body=%wide.region_1.2_spmd.clone.sunk | while | flops 524291 | bytes 2622240 | solution.py:107
  43.4 0.9 bitcast_dynamic-update-slice_fusion.2
  44.3 1.2 bitcast_add_fusion.2
  46.4 1.2 bitcast_add_fusion.2
  48.4 1.2 bitcast_add_fusion.2
  49.6 0.9 bitcast_dynamic-update-slice_fusion.2
  50.4 1.2 bitcast_add_fusion.2
  52.5 1.2 bitcast_add_fusion.2
  54.5 1.2 bitcast_add_fusion.2
  56.5 1.2 bitcast_add_fusion.2
  58.6 1.2 bitcast_add_fusion.2
  61.4 3.5 collective-permute-start.1
  66.6 36.2 %all-reduce = f32[256]{0:T(256)S(1)} all-reduce(f32[256]{0:T(256)S(1)} %dynamic-update-slice), channel_id=2, replica_groups=mesh['ctx'=16,'head'=8] {'ctx'}, use_global_device_ids=true, to_apply=%add | all-reduce | flops 256 | bytes 2048
  103.4 3.9 %copy.92 = bf16[1024,1024]{0,1:T(8,128)(2,1)} copy(bf16[1024,1024]{1,0:T(8,128)(2,1)} %param.22) | data formatting | bytes 4194304 | tf_op args[3]
  108.0 1.6 copy-done.3
  109.6 3.0 copy.104
  112.8 3.5 fusion.21
  116.3 11.3 %fusion.4 = f32[8,16,64,128]{3,2,1,0:T(8,128)} fusion(f32[8,16,128]{2,1,0:T(8,128)S(1)} %copy.78, f32[8,16,128]{2,1,0:T(8,128)S(1)} %copy.76, f32[8,128,128]{2,1,0:T(8,128)S(1)} %fusion.61, pred[128,128]{1,0:T(8,128)(4,1)S(1)} %iota_compare_fusion, bf16[8,128,16,64]{1,0,3,2:T(8,128)(2,1)S(1)} %bitcast.169), kind=kOutput, calls=%fused_computation.11 | convolution fusion | flops 1621098496 | bytes 6963200 | tf_op jit(solution)/shard_map/cghqk,ckghp->cqghp/dot_general | solution.py:95
  127.7 4.4 %all-gather.7.cloned.1.call-done = f32[16,16,64,128]{3,2,1,0:T(8,128)} async-done(((f32[1,16,64,128]{3,2,1,0:T(8,128)}), f32[16,16,64,128]{3,2,1,0:T(8,128)}) %all-gather.7.cloned.1.call-update) | async-done | bytes 8388624 | tf_op jit(solution)/shard_map/all_gather | solution.py:115
  132.1 12.8 %fusion.2 = f32[16,1,64,128]{3,1,2,0:T(1,128)S(1)} fusion(f32[16,16,1,1]{0,2,3,1:T(1,128)S(1)} %copy.96, f32[16,16,64,128]{3,2,1,0:T(8,128)} %all-gather.7.cloned.1.call-done), kind=kOutput, calls=%fused_computation.9 | convolution fusion | flops 25165824 | bytes 8913920 | tf_op jit(solution)/shard_map/jgh,jghpn->ghpn/dot_general | solution.py:123
  145.0 5.2 %fusion.19 = f32[8,128,1,16,64]{1,4,3,0,2:T(8,128)S(1)} fusion(f32[8,16,64,128]{3,2,1,0:T(8,128)S(1)} %copy-done.6, f32[8,16,64,128]{3,2,1,0:T(8,128)} %fusion.4, f32[8,128,1,16,64]{1,0,4,3,2:T(8,128)S(1)} %bitcast.166, f32[16,64,128,1]{2,1,0,3:T(8,128)S(1)} %bitcast.177, bf16[8,128,128,1]{2,1,3,0:T(8,128)(2,1)S(1)} %bitcast.173, f32[16]{0:T(128)S(1)} %copy-done.17, ...), kind=kOutput, calls=%fused_computation.35 | convolution fusion | flops 1616904192 | bytes 17694784 | tf_op jit(solution)/shard_map/cqgn,ghpn->cqghp/dot_general | solution.py:126
  150.2 3.3 copy.91
  153.6 1.7 multiply_reduce_fusion.1
  155.3 2.0 copy-done.4
  157.4 11.5 %convolution_convert_fusion = bf16[1024,4096]{1,0:T(8,128)(2,1)} fusion(bf16[1024,4096]{1,0:T(8,128)(2,1)S(1)} %bitcast.191, f32[1024,1024]{0,1:T(8,128)S(1)} %get-tuple-element.84, f32[1024]{0:T(1024)S(1)} %convert_element_type.84, f32[1024]{0:T(1024)S(1)} %add_rsqrt_fusion), kind=kOutput, calls=%fused_computation.18 | convolution fusion | flops 8597274624 | bytes 20979712 | tf_op jit(solution)/shard_map/dot_general | solution.py:151
  168.9 1.1 copy-done.9
  169.9 3.4 tile.4
  173.3 5.9 %all-to-all-start = ((bf16[96,64,512]{2,1,0:T(8,128)(2,1)}), bf16[96,64,512]{2,1,0:T(8,128)(2,1)}, u32[]{:S(2)}, u32[]{:S(2)}) async-start(bf16[96,64,512]{2,1,0:T(8,128)(2,1)} %bitcast.165), calls=%async_computation.1 | async-start | bytes 12582912 | tf_op jit(solution)/shard_map/all_to_all | solution.py:54
  180.9 128.4 %all-to-all-done = bf16[96,64,512]{2,1,0:T(8,128)(2,1)} async-done(((bf16[96,64,512]{2,1,0:T(8,128)(2,1)}), bf16[96,64,512]{2,1,0:T(8,128)(2,1)}, u32[]{:S(2)}, u32[]{:S(2)}) %all-to-all-start) | async-done | bytes 6291488 | tf_op jit(solution)/shard_map/all_to_all | solution.py:54
  309.3 3.4 gather_fusion.3
  312.7 5.4 %gather_fusion.2 = bf16[3,1024,64]{1,2,0:T(8,128)(2,1)S(1)} fusion(bf16[96,1024,64]{1,2,0:T(8,128)(2,1)} %all-gather.5.cloned.1.call-done, s32[1024]{0:T(1024)S(1)} %pad_clamp_fusion), kind=kCustom, calls=%fused_computation.2 | custom fusion | bytes 786444 | tf_op jit(solution)/shard_map/jit(_take)/gather | solution.py:148
  318.2 2.9 fusion.59
  321.2 31.4 %all-reduce.2 = bf16[1024,64]{0,1:T(8,128)(2,1)S(1)} all-reduce(f32[1024,64]{0,1:T(8,128)S(1)} %multiply_reduce_fusion.2), channel_id=1, replica_groups=mesh['ctx'=16,'head'=8] {'head'}, use_global_device_ids=true, to_apply=%region_9.10 | all-reduce | flops 65536 | bytes 393216 | tf_op jit(solution)/shard_map/psum | solution.py:162
  352.7 1.0 multiply_reduce_fusion
  353.7 2.6 add_convert_fusion
  (120 shorter events, 15.5 us)
Async XLA Ops:
  6.5 172.8 %copy-start = (s32[32]{0:T(128)S(1)}, s32[32]{0:T(128)}, u32[]{:S(2)}) copy-start(s32[32]{0:T(128)} %param.34) | copy-start | bytes 388
  6.5 23.9 %copy-start.10 = (bf16[1024,128]{1,0:T(8,128)(2,1)S(1)}, bf16[1024,128]{1,0:T(8,128)(2,1)}, u32[]{:S(2)}) copy-start(bf16[1024,128]{1,0:T(8,128)(2,1)} %param.20) | copy-start | bytes 786436
  6.5 125.5 %all-gather.7.cloned.1.call-start = ((), (), s32[]{:S(2)}) async-start(), calls=%async_computation.4 | async-start | bytes 8912896 | tf_op jit(solution)/shard_map/all_gather | solution.py:115
  8.2 23.3 %collective-permute-start = (bf16[3,1024]{0,1:T(8,128)(2,1)}, bf16[3,1024]{0,1:T(8,128)(2,1)S(1)}, u32[]{:S(2)}, u32[]{:S(2)}) collective-permute-start(bf16[3,1024]{0,1:T(8,128)(2,1)} %copy.74), channel_id=1, source_target_pairs={{0,8},{8,16},{16,24},{24,32},{32,40},{40,48},{48,56},{56,64},{64,7... | collective-permute-start | bytes 18440 | tf_op jit(solution)/shard_map/ppermute | solution.py:18
  12.8 17.6 %collective-permute-start.2 = (bf16[3,128]{1,0:T(4,128)(2,1)S(1)}, bf16[3,128]{1,0:T(4,128)(2,1)S(1)}, u32[]{:S(2)}, u32[]{:S(2)}) collective-permute-start(bf16[3,128]{1,0:T(4,128)(2,1)S(1)} %slice.104), channel_id=1, source_target_pairs={{0,8},{8,16},{16,24},{24,32},{32,40},{40,48},{48,56},{56,64},{64,7... | collective-permute-start | bytes 2312 | tf_op jit(solution)/shard_map/ppermute | solution.py:18
  30.5 2.3 copy-start.13
  30.5 2.3 copy-start.14
  38.3 0.8 copy-start.12
  43.4 18.0 %copy-start.11 = (bf16[1024,128]{1,0:T(8,128)(2,1)S(1)}, bf16[1024,128]{1,0:T(8,128)(2,1)}, u32[]{:S(2)}) copy-start(bf16[1024,128]{1,0:T(8,128)(2,1)} %param.21) | copy-start | bytes 786436
  43.4 21.5 %copy-start.20 = (u32[128]{0:T(128)S(1)}, u32[128]{0:T(128)}, u32[]{:S(2)}) copy-start(u32[128]{0:T(128)} %constant.114) | copy-start | bytes 1540
  43.4 22.9 %copy-start.18 = (f32[16]{0:T(128)S(1)}, f32[16]{0:T(128)}, u32[]{:S(2)}) copy-start(f32[16]{0:T(128)} %get-tuple-element.89) | copy-start | bytes 196
  43.4 59.7 %copy-start.15 = (bf16[4,128]{1,0:T(4,128)(2,1)S(1)}, bf16[4,128]{1,0:T(4,128)(2,1)}, u32[]{:S(2)}) copy-start(bf16[4,128]{1,0:T(4,128)(2,1)} %param.28) | copy-start | bytes 3076
  59.7 0.8 copy-start.2
  59.8 47.5 %copy-start.16 = (bf16[1024]{0:T(1024)(128)(2,1)S(1)}, bf16[1024]{0:T(1024)(128)(2,1)}, u32[]{:S(2)}) copy-start(bf16[1024]{0:T(1024)(128)(2,1)} %param.29) | copy-start | bytes 6148
  60.6 252.1 %all-gather.5.cloned.1.call-start = ((), (), s32[]{:S(2)}) async-start(), calls=%async_computation.3 | async-start | bytes 13369344 | tf_op jit(solution)/shard_map/all_gather | solution.py:145
  61.3 292.4 %reduce-scatter.2.cloned.1.call-start = ((), (), s32[]{:S(2)}) async-start(), calls=%async_computation.2 | async-start | bytes 9437184 | tf_op jit(solution)/shard_map/reduce_scatter | solution.py:150
  61.4 45.9 %collective-permute-start.1 = (bf16[3,128]{1,0:T(4,128)(2,1)S(1)}, bf16[3,128]{1,0:T(4,128)(2,1)S(1)}, u32[]{:S(2)}, u32[]{:S(2)}) collective-permute-start(bf16[3,128]{1,0:T(4,128)(2,1)S(1)} %slice.95), channel_id=1, source_target_pairs={{0,8},{8,16},{16,24},{24,32},{32,40},{40,48},{48,56},{56,64},{64,7... | collective-permute-start | bytes 2312 | tf_op jit(solution)/shard_map/ppermute | solution.py:18
  107.3 2.3 copy-start.3
  109.6 3.2 copy-start.8
  127.7 17.3 %copy-start.17 = (f32[16]{0:T(128)S(1)}, f32[16]{0:T(128)}, u32[]{:S(2)}) copy-start(f32[16]{0:T(128)} %param.25) | copy-start | bytes 196
  132.1 12.9 %copy-start.5 = (f32[128,8,8,128]{3,2,1,0:T(8,128)S(1)}, f32[128,8,8,128]{3,2,1,0:T(8,128)}, u32[]{:S(2)}) copy-start(f32[128,8,8,128]{3,2,1,0:T(8,128)} %copy.104) | copy-start | bytes 12582916
  132.1 12.9 %copy-start.6 = (f32[8,16,64,128]{3,2,1,0:T(8,128)S(1)}, f32[8,16,64,128]{3,2,1,0:T(8,128)}, u32[]{:S(2)}) copy-start(f32[8,16,64,128]{3,2,1,0:T(8,128)} %fusion.21) | copy-start | bytes 12582916
  150.2 3.4 copy-start.7
  150.2 7.2 %slice-start = ((s8[8388608]{0:T(1024)(128)(4,1)}), s8[4194304]{0:T(1024)(128)(4,1)S(1)}, s32[]{:S(2)}) async-start(s8[8388608]{0:T(1024)(128)(4,1)} %bitcast.190), calls=%async_computation.5 | async-start | bytes 8388608
  153.5 3.8 %slice-start.1 = ((s8[8388608]{0:T(1024)(128)(4,1)}), s8[4194304]{0:T(1024)(128)(4,1)S(1)}, s32[]{:S(2)}) async-start(s8[8388608]{0:T(1024)(128)(4,1)} %bitcast.190), calls=%async_computation.6 | async-start | bytes 8388608
  155.3 2.1 copy-start.4
  168.8 1.1 copy-start.9
  173.3 6.7 %copy-start.1 = (s32[96]{0:T(128)S(1)}, s32[96]{0:T(128)}, u32[]{:S(2)}) copy-start(s32[96]{0:T(128)} %param.35) | copy-start | bytes 1156
  173.3 7.3 %copy-start.19 = (s32[32]{0:T(128)S(1)}, s32[32]{0:T(128)}, u32[]{:S(2)}) copy-start(s32[32]{0:T(128)} %param.33) | copy-start | bytes 388
  173.3 136.0 %all-to-all-start = ((bf16[96,64,512]{2,1,0:T(8,128)(2,1)}), bf16[96,64,512]{2,1,0:T(8,128)(2,1)}, u32[]{:S(2)}, u32[]{:S(2)}) async-start(bf16[96,64,512]{2,1,0:T(8,128)(2,1)} %bitcast.165), calls=%async_computation.1 | async-start | bytes 12582912 | tf_op jit(solution)/shard_map/all_to_all | solution.py:54
Sparse Core Ops, SparseCore 0:
  60.7 71.3 all-gather.6
  134.3 157.6 all-gather.4
  294.4 57.7 reduce-scatter.1
